TPU v7x, 32 devices: a whole 2x2x4 slice. The times are simulated.
32 devices in a mesh: node: 4 (over z), chip: 8 (over y, x, core).
Axes of the slice: x: 2, y: 2, z: 4, core: 2. Of those that a mesh axis runs over, the one named last changes fastest.
Arguments:
- tokens: bfloat16 [512, 3584], P(('node', 'chip')), may hold values from -6 to 6
- expert_ids: int32 [512, 8], P(('node', 'chip')), may hold values from 0 to 31, all different within a row; in each aligned block of 16 rows (0 to 15, 16 to 31, ...) at most 8 rows name the same one
- route_weight: float32 [512, 8], P(('node', 'chip')), may hold values from 0.1 to 1
- expert_gate: bfloat16 [32, 3584, 1024], P(('node', 'chip')), may hold values from -0.09375 to 0.09375
- expert_up: bfloat16 [32, 3584, 1024], P(('node', 'chip')), may hold values from -0.09375 to 0.09375
- expert_down: bfloat16 [32, 1024, 3584], P(('node', 'chip')), may hold values from -0.1875 to 0.1875
- shared_gate: bfloat16 [3584, 2048], P(None, 'chip'), may hold values from -0.09375 to 0.09375
- shared_up: bfloat16 [3584, 2048], P(None, 'chip'), may hold values from -0.09375 to 0.09375
- shared_down: bfloat16 [2048, 3584], P('chip'), may hold values from -0.125 to 0.125
- query_latent: bfloat16 [128, 64, 512], P(('node', 'chip')), may hold values from -32 to 32
- query_rope: bfloat16 [128, 4096], P(('node', 'chip')), may hold values from -4 to 4
- cache_latent: bfloat16 [128, 128, 512], P(('node', 'chip')), may hold values from -8 to 8
- cache_rope: bfloat16 [128, 64, 128], P(('node', 'chip')), may hold values from -4 to 4
- cache_len: int32 [128], P(('node', 'chip')), may hold values from 2 to 128
Outputs:
- moe_out: bfloat16 [512, 3584], P(('node', 'chip'))
- attn_out: bfloat16 [128, 64, 512], P(('node', 'chip'))
Inputs may be any that keep to these rules, and one draw needn't show every extreme that they name: `expert_ids`: a row names 8 different experts; the rows of one device name any one expert at most 8 times, a bound that some block reaches.
All inputs are finite; a program needn't handle non-finite values.
Results may differ from a plain program's by a relative error of at most 0.0085.
Values may be sent and summed in bfloat16 or wider, within the bound.
A program may use at most 128 MiB of HBM per device.

v0:
```python
import jax
import jax.numpy as jnp
from jax import lax
from jax.sharding import PartitionSpec as P

TOPK = 8


score_scale = 192.0 ** (-0.5)


def swiglu_hidden(token_rows, gate_matrix, up_matrix):
    gate_part = jnp.dot(token_rows, gate_matrix, preferred_element_type=jnp.float32)
    up_part = jnp.dot(token_rows, up_matrix, preferred_element_type=jnp.float32)
    return (jax.nn.silu(gate_part) * up_part).astype(jnp.bfloat16)


def attend(query_latent, query_rope, cache_latent, cache_rope, cache_len):
    seq_count, head_count, latent_width = query_latent.shape
    rope_width = cache_rope.shape[1]
    cache_size = cache_rope.shape[2]
    rope_query = query_rope.reshape(seq_count, head_count, rope_width)
    scores = jnp.einsum(
        "shl,spl->shp", query_latent, cache_latent, preferred_element_type=jnp.float32
    )
    scores = scores + jnp.einsum(
        "shr,srp->shp", rope_query, cache_rope, preferred_element_type=jnp.float32
    )
    scores = scores * score_scale
    position = jnp.arange(cache_size, dtype=jnp.int32)
    live_mask = position[None, None, :] < cache_len[:, None, None]
    masked = jnp.where(live_mask, scores, -1e30)
    row_peak = jnp.max(masked, axis=2, keepdims=True)
    weight = jnp.where(live_mask, jnp.exp(masked - row_peak), 0.0)
    softmax_weight = (weight / jnp.sum(weight, axis=2, keepdims=True)).astype(jnp.bfloat16)
    attended = jnp.einsum(
        "shp,spl->shl", softmax_weight, cache_latent, preferred_element_type=jnp.float32
    )
    return attended.astype(jnp.bfloat16)


def local(
    tokens,
    expert_ids,
    route_weight,
    expert_gate,
    expert_up,
    expert_down,
    shared_gate,
    shared_up,
    shared_down,
    query_latent,
    query_rope,
    cache_latent,
    cache_rope,
    cache_len,
):
    node_count = lax.axis_size("node")
    chip_count = lax.axis_size("chip")
    experts = node_count * chip_count
    tok_rows, model_width = tokens.shape
    slots = (2 * tok_rows * TOPK + experts - 1) // experts
    flat_ids = expert_ids.reshape(-1)
    onehot = (flat_ids[:, None] == jnp.arange(experts, dtype=jnp.int32)[None, :]).astype(jnp.int32)
    earlier = jnp.cumsum(onehot, axis=0) - onehot
    slot_index = jnp.sum(earlier * onehot, axis=1)
    target_slot = flat_ids * slots + slot_index
    repeated = jnp.repeat(tokens, TOPK, axis=0)
    outgoing = jnp.zeros((experts * slots, model_width), jnp.bfloat16).at[target_slot].set(repeated)
    outgoing = outgoing.reshape(experts, slots, model_width)
    gate_matrix = expert_gate[0]
    up_matrix = expert_up[0]
    down_matrix = expert_down[0]
    received = lax.all_to_all(outgoing, ("node", "chip"), split_axis=0, concat_axis=0, tiled=True)
    flat_rows = received.reshape(-1, model_width)
    hidden = swiglu_hidden(flat_rows, gate_matrix, up_matrix)
    result = jnp.dot(hidden, down_matrix, preferred_element_type=jnp.float32).astype(jnp.bfloat16)
    returned = lax.all_to_all(
        result.reshape(received.shape), ("node", "chip"), split_axis=0, concat_axis=0, tiled=True
    )
    flat_back = returned.reshape(experts * slots, model_width)
    picked = flat_back[target_slot].reshape(tok_rows, TOPK, model_width)
    routed = jnp.sum(route_weight[:, :, None] * picked.astype(jnp.float32), axis=1)
    hidden = swiglu_hidden(
        lax.all_gather(tokens, "chip", axis=0, tiled=True), shared_gate, shared_up
    )
    partial_terms = jnp.dot(hidden, shared_down, preferred_element_type=jnp.float32)
    shared = lax.psum_scatter(partial_terms, "chip", scatter_dimension=0, tiled=True)
    moe_out = (shared + routed).astype(jnp.bfloat16)
    attn_out = attend(query_latent, query_rope, cache_latent, cache_rope, cache_len)
    return (moe_out, attn_out)


def solution(mesh):
    placed = (
        P(("node", "chip"), None),
        P(("node", "chip"), None),
        P(("node", "chip"), None),
        P(("node", "chip"), None, None),
        P(("node", "chip"), None, None),
        P(("node", "chip"), None, None),
        P(None, "chip"),
        P(None, "chip"),
        P("chip", None),
        P(("node", "chip"), None, None),
        P(("node", "chip"), None),
        P(("node", "chip"), None, None),
        P(("node", "chip"), None, None),
        P(("node", "chip")),
    )
    return jax.shard_map(
        local,
        mesh=mesh,
        in_specs=placed,
        out_specs=(P(("node", "chip"), None), P(("node", "chip"), None, None)),
        check_vma=False,
    )
```

profile of v0, /device:TPU:9, one launch (start us, length us, event | category | flops | bytes accessed | tf_op | source)
XLA Modules:
  0.0 161.8 jit_solution(5306558353606883719)
XLA Ops:
  7.2 0.9 copy.21
  8.1 0.7 broadcast_multiply_fusion
  8.9 0.2 reduce_window_sum.11
  9.1 0.2 select_reduce_fusion
  9.5 3.7 %scatter_custom_fusion = bf16[256,3584]{1,0:T(8,128)(2,1)} fusion(s32[128]{0:T(128)S(1)} %fusion.50, bf16[]{:T(256)} %constant.5.clone.1, bf16[16,3584]{1,0:T(8,128)(2,1)} %param.14), kind=kCustom, calls=%fused_computation.27 | custom fusion | bytes 1949698 | tf_op jit(solution)/shard_map/scatter | solution.py:69
  13.2 48.8 %all_to_all.10 = bf16[32,8,3584]{2,1,0:T(8,128)(2,1)S(1)} all-to-all(bf16[32,8,3584]{2,1,0:T(8,128)(2,1)} %bitcast.58), channel_id=1, replica_groups=mesh['node'=4,'chip'=8] {'node','chip'}, dimensions={0} | all-to-all | bytes 3670016 | tf_op jit(solution)/shard_map/all_to_all | solution.py:74
  62.0 1.2 copy-done.1
  63.3 5.1 %fusion.5 = f32[256,1024]{1,0:T(8,128)S(1)} fusion(bf16[1,3584,1024]{2,1,0:T(8,128)(2,1)} %param.17, bf16[32,8,3584]{2,1,0:T(8,128)(2,1)S(1)} %all_to_all.10), kind=kOutput, calls=%fused_computation.7 | convolution fusion | flops 1879048192 | bytes 10223616 | tf_op jit(solution)/shard_map/dot_general | solution.py:13
  68.4 11.0 %fusion.10 = bf16[32,8,3584]{2,1,0:T(8,128)(2,1)} fusion(bf16[1,1024,3584]{2,1,0:T(8,128)(2,1)} %param.19, bf16[1,3584,1024]{2,1,0:T(8,128)(2,1)} %param.18, bf16[32,8,3584]{2,1,0:T(8,128)(2,1)} %copy-done.1, f32[256,1024]{1,0:T(8,128)S(1)} %fusion.5), kind=kOutput, calls=%fused_computation.10 | convolution fusion | flops 3760586752 | bytes 19398656 | tf_op jit(solution)/shard_map/dot_general | solution.py:77
  79.4 4.2 %all-to-all-start.1 = ((bf16[32,8,3584]{2,1,0:T(8,128)(2,1)}), bf16[32,8,3584]{2,1,0:T(8,128)(2,1)}, u32[]{:S(2)}, u32[]{:S(2)}) async-start(bf16[32,8,3584]{2,1,0:T(8,128)(2,1)} %fusion.10), calls=%async_computation.2 | async-start | bytes 3670016 | tf_op jit(solution)/shard_map/all_to_all | solution.py:78
  83.7 20.8 %all_gather.3 = bf16[128,3584]{1,0:T(8,128)(2,1)S(1)} all-gather(bf16[16,3584]{1,0:T(8,128)(2,1)S(1)} %copy-done.3), channel_id=1, replica_groups=mesh['node'=4,'chip'=8] {'chip'}, dimensions={0}, use_global_device_ids=true | all-gather | bytes 1032192 | tf_op jit(solution)/shard_map/all_gather | solution.py:85
  104.5 1.9 %fusion.56 = f32[128,256]{1,0:T(8,128)S(1)} fusion(bf16[128,3584]{1,0:T(8,128)(2,1)S(1)} %all_gather.3, bf16[3584,256]{1,0:T(8,128)(2,1)} %param.20), kind=kOutput, calls=%fused_computation.55 | convolution fusion | flops 234881024 | bytes 2883584 | tf_op jit(solution)/shard_map/dot_general | solution.py:13
  106.4 3.9 %fusion.32 = f32[128,3584]{1,0:T(8,128)} fusion(bf16[256,3584]{1,0:T(8,128)(2,1)S(1)} %copy-done, bf16[128,3584]{1,0:T(8,128)(2,1)S(1)} %all_gather.3, bf16[3584,256]{1,0:T(8,128)(2,1)} %param.21, f32[128,256]{1,0:T(8,128)S(1)} %fusion.56), kind=kOutput, calls=%fused_computation.26 | convolution fusion | flops 469958656 | bytes 6553600 | tf_op jit(solution)/shard_map/dot_general | solution.py:87
  110.4 0.6 copy-done.7
  111.1 0.1 reshape.84
  111.4 0.1 fusion.57
  111.6 0.3 fusion.28
  111.9 0.2 fusion.55
  112.1 1.3 convolution_convert_fusion
  113.3 12.1 %all-to-all-done.1 = bf16[32,8,3584]{2,1,0:T(8,128)(2,1)} async-done(((bf16[32,8,3584]{2,1,0:T(8,128)(2,1)}), bf16[32,8,3584]{2,1,0:T(8,128)(2,1)}, u32[]{:S(2)}, u32[]{:S(2)}) %all-to-all-start.1) | async-done | bytes 1835040 | tf_op jit(solution)/shard_map/all_to_all | solution.py:78
  125.5 3.8 %gather_fusion = bf16[128,3584]{1,0:T(8,128)(2,1)S(1)} fusion(bf16[256,3584]{1,0:T(8,128)(2,1)} %bitcast.9, s32[1024]{0:T(1024)S(1)} %pad_clamp_fusion), kind=kCustom, calls=%fused_computation | custom fusion | bytes 1835520 | tf_op jit(solution)/shard_map/gather | solution.py:82
  129.3 0.7 fusion.13
  130.0 23.3 %reduce-scatter.2.cloned.1.call-done = f32[16,3584]{1,0:T(8,128)} async-done(((f32[128,3584]{1,0:T(8,128)}), f32[16,3584]{1,0:T(8,128)}) %reduce-scatter.2.cloned.1.call-update) | async-done | bytes 229392 | tf_op jit(solution)/shard_map/reduce_scatter | solution.py:88
  153.3 1.6 add_convert_fusion
  (26 shorter events, 0.7 us)
Async XLA Ops:
  7.2 99.3 %copy-start = (bf16[256,3584]{1,0:T(8,128)(2,1)S(1)}, bf16[256,3584]{1,0:T(8,128)(2,1)}, u32[]{:S(2)}) copy-start(bf16[256,3584]{1,0:T(8,128)(2,1)} %param.22) | copy-start | bytes 5505028
  62.0 1.2 copy-start.1
  79.4 4.3 %copy-start.3 = (bf16[16,3584]{1,0:T(8,128)(2,1)S(1)}, bf16[16,3584]{1,0:T(8,128)(2,1)}, u32[]{:S(2)}) copy-start(bf16[16,3584]{1,0:T(8,128)(2,1)} %param.14) | copy-start | bytes 344068
  79.4 46.1 %all-to-all-start.1 = ((bf16[32,8,3584]{2,1,0:T(8,128)(2,1)}), bf16[32,8,3584]{2,1,0:T(8,128)(2,1)}, u32[]{:S(2)}, u32[]{:S(2)}) async-start(bf16[32,8,3584]{2,1,0:T(8,128)(2,1)} %fusion.10), calls=%async_computation.2 | async-start | bytes 3670016 | tf_op jit(solution)/shard_map/all_to_all | solution.py:78
  83.6 69.7 %reduce-scatter.2.cloned.1.call-start = ((), (), s32[]{:S(2)}) async-start(), calls=%async_computation.3 | async-start | bytes 2064384 | tf_op jit(solution)/shard_map/reduce_scatter | solution.py:88
  110.4 0.7 copy-start.7
  110.4 0.8 copy-start.6
  110.4 0.9 copy-start.8
  110.4 1.0 copy-start.5
  110.4 1.1 copy-start.2
  110.4 1.2 copy-start.4
Sparse Core Ops, SparseCore 0:
  110.5 42.7 reduce-scatter.1
where the time goes:
time: 164 us; the launch traced here: 162 us
  blocking collectives  69.7 us (42%)
  waiting for transfers between devices  35.4 us (22%)
  matrix products  23.7 us (14%)
  between operations  14.2 us (9%)
  local copies, waits for them, and re-layouts  10.8 us (7%)
  starting transfers between devices  4.26 us (3%)
  other arithmetic  3.7 us (2%)
    all_to_all x1, blocking collectives, local(): lax.all_to_all(outgoing, ('node', 'chip'), split_axis=0, concat_axis=0, t...  48.8 us
    reduce_scatter x1, waiting for transfers between devices, local(): lax.psum_scatter(partial_terms, 'chip', scatter_dimension=0, tiled=True)  23.3 us
    all_gather x1, blocking collectives, local(): lax.all_gather(tokens, 'chip', axis=0, tiled=True)  20.8 us
    all_to_all x1, waiting for transfers between devices, local(): lax.all_to_all(result.reshape(received.shape), ('node', 'chip'), split_ax...  12.1 us
    dot_general x1, matrix products, local(): jnp.dot(hidden, down_matrix, preferred_element_type=jnp.float32)  11 us
    dot_general x2, matrix products, swiglu_hidden(): jnp.dot(token_rows, gate_matrix, preferred_element_type=jnp.float32)  7.04 us
    all_to_all x1, starting transfers between devices, local(): lax.all_to_all(result.reshape(received.shape), ('node', 'chip'), split_ax...  4.22 us
    dot_general x1, matrix products, local(): jnp.dot(hidden, shared_down, preferred_element_type=jnp.float32)  3.94 us
  transfers between devices with their start and end apart: 2, of which 2 were waited for; matrix products, arithmetic and copies ran while one was open for 8% of the time, Pallas kernels for 0%

commit v1 on v0

--- a/solution.py
+++ b/solution.py
@@ -1,9 +1,12 @@
 import jax
 import jax.numpy as jnp
 from jax import lax
+from jax.experimental import pallas as pl
+from jax.experimental.pallas import tpu as pltpu
 from jax.sharding import PartitionSpec as P
 
-TOPK = 8
+MESH = pl.DeviceIdType.MESH
+LANES = 128
 
 
 score_scale = 192.0 ** (-0.5)
@@ -37,6 +40,255 @@
         "shp,spl->shl", softmax_weight, cache_latent, preferred_element_type=jnp.float32
     )
     return attended.astype(jnp.bfloat16)
+
+
+class Place:
+    def __init__(self, nodes):
+        self.nodes = nodes
+        self.z = lax.axis_index("node")
+        chip = lax.axis_index("chip")
+        self.y, self.x, self.c = chip // 4, (chip // 2) % 2, chip % 2
+
+    def block(self, z, y, x, c):
+        return z * 8 + y * 4 + x * 2 + c
+
+    def dev(self, z=None, y=None, x=None, c=None):
+        pick = lambda new, own: own if new is None else new
+        chip = pick(y, self.y) * 4 + pick(x, self.x) * 2 + pick(c, self.c)
+        return {"node": pick(z, self.z), "chip": chip}
+
+    def other_z(self, step):
+        return lax.rem(self.z + step, self.nodes)
+
+    def partners(self):
+        found = [self.dev(z=self.other_z(s)) for s in range(1, self.nodes)]
+        return found + [self.dev(y=1 - self.y), self.dev(x=1 - self.x), self.dev(c=1 - self.c)]
+
+
+def greet(place):
+    barrier = pltpu.get_barrier_semaphore()
+    partners = place.partners()
+    for who in partners:
+        pl.semaphore_signal(barrier, inc=1, device_id=who, device_id_type=MESH)
+    pl.semaphore_wait(barrier, len(partners))
+
+
+def gather_kernel(nodes, own_ref, out_ref, held, z_send, z_recv, xy_send, xy_recv, c_send, c_recv,
+                  own_sem, out_sem):
+    p = Place(nodes)
+    width = held.shape[2]
+    half = width // LANES // 2 * LANES
+    cols = (pl.ds(0, half), pl.ds(half, width - half))
+    me = p.block(p.z, p.y, p.x, p.c)
+    load = pltpu.make_async_copy(own_ref, held.at[me], own_sem)
+    load.start()
+    greet(p)
+    load.wait()
+    sends, outs = [], []
+
+    def copy(block, h, send, recv, who):
+        return pltpu.make_async_remote_copy(
+            held.at[block, :, cols[h]], held.at[block, :, cols[h]], send, recv,
+            device_id=who, device_id_type=MESH)
+
+    def push(block, h, send, recv, who):
+        one = copy(block, h, send, recv, who)
+        one.start()
+        sends.append(one)
+
+    def arrive(block, h, sem):
+        copy(block, h, sem, sem, p.dev(c=1 - p.c)).wait_recv()
+
+    def keep(block, h):
+        n = len(outs)
+        one = pltpu.make_async_copy(
+            held.at[block, :, cols[h]], out_ref.at[block, :, cols[h]], out_sem.at[n])
+        one.start()
+        outs.append(one)
+
+    def near(h):
+        return (p.dev(x=1 - p.x), p.dev(y=1 - p.y))[h]
+
+    def far(h):
+        return (p.dev(y=1 - p.y), p.dev(x=1 - p.x))[h]
+
+    def far_source(h, z, k):
+        if h == 0:
+            return p.block(z, 1 - p.y, (p.x, 1 - p.x)[k], p.c)
+        return p.block(z, (p.y, 1 - p.y)[k], 1 - p.x, p.c)
+
+    def near_source(h, z):
+        return p.block(z, p.y, 1 - p.x, p.c) if h == 0 else p.block(z, 1 - p.y, p.x, p.c)
+
+    def to_core(block, h, n):
+        push(block, h, c_send.at[h, n], c_recv.at[h, n], p.dev(c=1 - p.c))
+        keep(block, h)
+
+    order = [0] + [s for pair in zip(range(1, nodes), range(nodes - 1, 0, -1)) for s in pair]
+    order = list(dict.fromkeys(order))
+    for s in order[1:]:
+        for h in range(2):
+            push(me, h, z_send.at[h, s], z_recv.at[h, s], p.dev(z=p.other_z(s)))
+    for s in order:
+        z_from = lax.rem(p.z + nodes - s, nodes)
+        block = p.block(z_from, p.y, p.x, p.c)
+        for h in range(2):
+            if s:
+                arrive(block, h, z_recv.at[h, s])
+            push(block, h, xy_send.at[h, 0, s], xy_recv.at[h, 0, s], near(h))
+            push(block, h, xy_send.at[h, 1, s], xy_recv.at[h, 1, s], far(h))
+            to_core(block, h, s)
+    for s in order:
+        z_from = lax.rem(p.z + nodes - s, nodes)
+        for h in range(2):
+            block = near_source(h, z_from)
+            arrive(block, h, xy_recv.at[h, 0, s])
+            push(block, h, xy_send.at[h, 2, s], xy_recv.at[h, 2, s], far(h))
+            to_core(block, h, nodes + s)
+        for h in range(2):
+            block = far_source(h, z_from, 0)
+            arrive(block, h, xy_recv.at[h, 1, s])
+            to_core(block, h, 2 * nodes + s)
+    for s in order:
+        z_from = lax.rem(p.z + nodes - s, nodes)
+        for h in range(2):
+            block = far_source(h, z_from, 1)
+            arrive(block, h, xy_recv.at[h, 2, s])
+            to_core(block, h, 3 * nodes + s)
+    for s in order:
+        z_from = lax.rem(p.z + nodes - s, nodes)
+        for h in range(2):
+            core = lambda y, x: p.block(z_from, y, x, 1 - p.c)
+            near_at = (p.y, 1 - p.x) if h == 0 else (1 - p.y, p.x)
+            far_at = (1 - p.y, p.x) if h == 0 else (p.y, 1 - p.x)
+            spots = ((p.y, p.x), near_at, far_at, (1 - p.y, 1 - p.x))
+            for k, (y, x) in enumerate(spots):
+                block = core(y, x)
+                arrive(block, h, c_recv.at[h, k * nodes + s])
+                keep(block, h)
+    for one in sends:
+        one.wait_send()
+    for one in outs:
+        one.wait()
+
+
+def gather_tokens(rows, nodes):
+    count, width = rows.shape
+    devices = nodes * 8
+    dma = pltpu.SemaphoreType.DMA
+    return pl.pallas_call(
+        lambda *refs: gather_kernel(nodes, *refs),
+        out_shape=jax.ShapeDtypeStruct((devices, count, width), rows.dtype),
+        in_specs=[pl.BlockSpec(memory_space=pl.ANY)],
+        out_specs=pl.BlockSpec(memory_space=pl.ANY),
+        scratch_shapes=[
+            pltpu.VMEM((devices, count, width), rows.dtype),
+            dma((2, nodes)), dma((2, nodes)),
+            dma((2, 3, nodes)), dma((2, 3, nodes)),
+            dma((2, 4 * nodes)), dma((2, 4 * nodes)),
+            dma, dma((2 * devices,)),
+        ],
+        compiler_params=pltpu.CompilerParams(collective_id=0, has_side_effects=True),
+        name="gather_tokens",
+    )(rows)
+
+
+def scatter_kernel(nodes, in_ref, out_ref, mine, r1, r2, r3, r4, s1, t1, s2, t2, s3, t3, s4, t4,
+                   in_sem):
+    p = Place(nodes)
+    width = mine.shape[2]
+    half = width // LANES // 2 * LANES
+    cols = (pl.ds(0, half), pl.ds(half, width - half))
+    loads = []
+    order = list(range(1, nodes)) + [0]
+    spots = {0: ((1, 1), (1, 0), (0, 1), (0, 0)), 1: ((1, 1), (0, 1), (1, 0), (0, 0))}
+    sequence = [(h, k, s) for k in range(4) for s in order for h in range(2)]
+
+    def at(h, k, s, c):
+        fy, fx = spots[h][k]
+        y = 1 - p.y if fy else p.y
+        x = 1 - p.x if fx else p.x
+        return p.block(p.other_z(s), y, x, c)
+
+    for n, (h, k, s) in enumerate(sequence):
+        for own in range(2):
+            block = at(h, k, s, p.c if own else 1 - p.c)
+            load = pltpu.make_async_copy(
+                in_ref.at[block, :, cols[h]], mine.at[block, :, cols[h]], in_sem.at[own, n])
+            load.start()
+            loads.append(load)
+    greet(p)
+    sends = []
+
+    def push(src, dst, send, recv, who):
+        one = pltpu.make_async_remote_copy(src, dst, send, recv, device_id=who, device_id_type=MESH)
+        one.start()
+        sends.append(one)
+
+    def arrive(dst, recv):
+        pltpu.make_async_remote_copy(
+            dst, dst, recv, recv, device_id=p.dev(c=1 - p.c), device_id_type=MESH).wait_recv()
+
+    def plus(first, second):
+        return first.astype(jnp.float32) + second.astype(jnp.float32)
+
+    first_link = (p.dev(y=1 - p.y), p.dev(x=1 - p.x))
+    second_link = (p.dev(x=1 - p.x), p.dev(y=1 - p.y))
+    for n, (h, k, s) in enumerate(sequence):
+        loads[2 * n].wait()
+        push(mine.at[at(h, k, s, 1 - p.c), :, cols[h]], r1.at[h, k, s], s1.at[h, k, s],
+             t1.at[h, k, s], p.dev(c=1 - p.c))
+    for n, (h, k, s) in enumerate(sequence):
+        loads[2 * n + 1].wait()
+        arrive(r1.at[h, k, s], t1.at[h, k, s])
+        r1[h, k, s] = plus(r1[h, k, s], mine[at(h, k, s, p.c), :, cols[h]]).astype(jnp.bfloat16)
+        if k < 2:
+            push(r1.at[h, k, s], r2.at[h, k, s], s2.at[h, k, s], t2.at[h, k, s], first_link[h])
+    for s in order:
+        for h in range(2):
+            arrive(r2.at[h, 0, s], t2.at[h, 0, s])
+            r2[h, 0, s] = plus(r2[h, 0, s], r1[h, 2, s]).astype(jnp.bfloat16)
+            push(r2.at[h, 0, s], r3.at[h, s], s3.at[h, s], t3.at[h, s], second_link[h])
+    for s in order:
+        for h in range(2):
+            arrive(r2.at[h, 1, s], t2.at[h, 1, s])
+            arrive(r3.at[h, s], t3.at[h, s])
+            total = plus(r2[h, 1, s], r1[h, 3, s]) + r3[h, s].astype(jnp.float32)
+            r3[h, s] = total.astype(jnp.bfloat16)
+            if s:
+                push(r3.at[h, s], r4.at[h, s], s4.at[h, s], t4.at[h, s], p.dev(z=p.other_z(s)))
+    for h in range(2):
+        total = r3[h, 0].astype(jnp.float32)
+        for s in range(1, nodes):
+            arrive(r4.at[h, s], t4.at[h, s])
+            total = total + r4[h, s].astype(jnp.float32)
+        out_ref[:, cols[h]] = total.astype(jnp.bfloat16)
+    for one in sends:
+        one.wait_send()
+
+
+def scatter_sums(terms, nodes):
+    devices, count, width = terms.shape
+    half = width // 2
+    dma = pltpu.SemaphoreType.DMA
+    vmem = lambda *lead: pltpu.VMEM((*lead, count, half), terms.dtype)
+    return pl.pallas_call(
+        lambda *refs: scatter_kernel(nodes, *refs),
+        out_shape=jax.ShapeDtypeStruct((count, width), terms.dtype),
+        in_specs=[pl.BlockSpec(memory_space=pl.ANY)],
+        out_specs=pl.BlockSpec(memory_space=pltpu.VMEM),
+        scratch_shapes=[
+            pltpu.VMEM((devices, count, width), terms.dtype),
+            vmem(2, 4, nodes), vmem(2, 2, nodes), vmem(2, nodes), vmem(2, nodes),
+            dma((2, 4, nodes)), dma((2, 4, nodes)),
+            dma((2, 2, nodes)), dma((2, 2, nodes)),
+            dma((2, nodes)), dma((2, nodes)),
+            dma((2, nodes)), dma((2, nodes)),
+            dma((2, devices)),
+        ],
+        compiler_params=pltpu.CompilerParams(collective_id=1, has_side_effects=True),
+        name="scatter_sums",
+    )(terms)
 
 
 def local(
@@ -59,34 +311,58 @@
     chip_count = lax.axis_size("chip")
     experts = node_count * chip_count
     tok_rows, model_width = tokens.shape
-    slots = (2 * tok_rows * TOPK + experts - 1) // experts
-    flat_ids = expert_ids.reshape(-1)
-    onehot = (flat_ids[:, None] == jnp.arange(experts, dtype=jnp.int32)[None, :]).astype(jnp.int32)
-    earlier = jnp.cumsum(onehot, axis=0) - onehot
-    slot_index = jnp.sum(earlier * onehot, axis=1)
-    target_slot = flat_ids * slots + slot_index
-    repeated = jnp.repeat(tokens, TOPK, axis=0)
-    outgoing = jnp.zeros((experts * slots, model_width), jnp.bfloat16).at[target_slot].set(repeated)
-    outgoing = outgoing.reshape(experts, slots, model_width)
-    gate_matrix = expert_gate[0]
-    up_matrix = expert_up[0]
-    down_matrix = expert_down[0]
-    received = lax.all_to_all(outgoing, ("node", "chip"), split_axis=0, concat_axis=0, tiled=True)
-    flat_rows = received.reshape(-1, model_width)
-    hidden = swiglu_hidden(flat_rows, gate_matrix, up_matrix)
-    result = jnp.dot(hidden, down_matrix, preferred_element_type=jnp.float32).astype(jnp.bfloat16)
-    returned = lax.all_to_all(
-        result.reshape(received.shape), ("node", "chip"), split_axis=0, concat_axis=0, tiled=True
-    )
-    flat_back = returned.reshape(experts * slots, model_width)
-    picked = flat_back[target_slot].reshape(tok_rows, TOPK, model_width)
-    routed = jnp.sum(route_weight[:, :, None] * picked.astype(jnp.float32), axis=1)
-    hidden = swiglu_hidden(
-        lax.all_gather(tokens, "chip", axis=0, tiled=True), shared_gate, shared_up
-    )
-    partial_terms = jnp.dot(hidden, shared_down, preferred_element_type=jnp.float32)
-    shared = lax.psum_scatter(partial_terms, "chip", scatter_dimension=0, tiled=True)
-    moe_out = (shared + routed).astype(jnp.bfloat16)
+    top = expert_ids.shape[1]
+    slots = (2 * tok_rows * top + experts - 1) // experts
+    trees = chip_count == 8
+    node, chip = lax.axis_index("node"), lax.axis_index("chip")
+    me = node * chip_count + chip
+
+    names = jnp.arange(experts, dtype=jnp.int32)
+    dense = jnp.sum(
+        jnp.where(expert_ids[:, :, None] == names, route_weight[:, :, None], 0.0), axis=1
+    )
+    high = lax.reduce_precision(dense, 8, 7)
+    low = dense - high
+    side = jnp.concatenate([high, low], axis=1).astype(jnp.bfloat16)
+    side = jnp.pad(side, ((0, 0), (0, -(2 * experts) % LANES)))
+    rows = jnp.concatenate([tokens, side], axis=1)
+    if trees:
+        gathered = gather_tokens(rows, node_count)
+    else:
+        gathered = lax.all_gather(rows, ("node", "chip"), axis=0)
+    total = experts * tok_rows
+    flat = gathered.reshape(total, -1)
+    every = flat[:, :model_width]
+    tail = flat[:, model_width:].astype(jnp.float32)
+    lane = lax.broadcasted_iota(jnp.int32, (1, tail.shape[1]), 1)
+    scale = jnp.sum(jnp.where((lane == me) | (lane == experts + me), tail, 0.0), axis=1)
+
+    chosen = (scale > 0).reshape(experts, tok_rows)
+    rank = jnp.cumsum(chosen.astype(jnp.int32), axis=1) - 1
+    slot = jnp.where(chosen, rank + slots * names[:, None], -1).reshape(-1)
+    place = (jnp.arange(experts * slots, dtype=jnp.int32)[:, None] == slot[None, :])
+    place = place.astype(jnp.bfloat16)
+    picked = jnp.dot(place, every, preferred_element_type=jnp.float32).astype(jnp.bfloat16)
+    hidden = swiglu_hidden(picked, expert_gate[0], expert_up[0])
+    result = jnp.dot(hidden, expert_down[0], preferred_element_type=jnp.float32)
+    result = result.astype(jnp.bfloat16)
+    spread = lax.dot_general(
+        place, result, (((0,), (0,)), ((), ())), preferred_element_type=jnp.float32
+    )
+    group = lax.dynamic_slice_in_dim(every, node * chip_count * tok_rows, chip_count * tok_rows, 0)
+    shared_hidden = swiglu_hidden(group, shared_gate, shared_up)
+    partial_terms = jnp.dot(shared_hidden, shared_down, preferred_element_type=jnp.float32)
+    in_group = (names // chip_count == node).astype(jnp.float32)
+    terms = (spread * scale[:, None]).reshape(node_count, -1, model_width)
+    own_node = jnp.arange(node_count) == node
+    terms = terms + jnp.where(own_node[:, None, None], partial_terms[None], 0.0)
+    terms = terms.astype(jnp.bfloat16).reshape(experts, tok_rows, model_width)
+    if trees:
+        moe_out = scatter_sums(terms, node_count)
+    else:
+        moe_out = lax.psum_scatter(
+            terms.reshape(total, model_width), ("node", "chip"), scatter_dimension=0, tiled=True
+        )
     attn_out = attend(query_latent, query_rope, cache_latent, cache_rope, cache_len)
     return (moe_out, attn_out)
 

time: 164 us -> 110 us (0.67); the launches traced: 162 us -> 110 us
  blocking collectives: 69.7 us -> 0 us
  Pallas kernels: 0 us -> 57.1 us
  waiting for transfers between devices: 35.4 us -> 0 us
  between operations: 14.2 us -> 0.85 us
  other arithmetic: 3.7 us -> 12.1 us
  starting transfers between devices: 4.26 us -> 0 us
  matrix products: 23.7 us -> 26.4 us
  local copies, waits for them, and re-layouts: 10.8 us -> 13.4 us
    pallas_call x0 -> x2, Pallas kernels: none -> 57.1 us  [the longest x1 31.9 us: scatter_sums(): pl.pallas_call(lambda *refs: scatter_kernel(nodes, *refs), out_shape=jax....]
    all_to_all x1 -> x0, blocking collectives: 48.8 us -> none  [local(): lax.all_to_all(outgoing, ('node', 'chip'), split_axis=0, concat_axis=0, t...]
    reduce_scatter x1 -> x0, waiting for transfers between devices: 23.3 us -> none  [local(): lax.psum_scatter(partial_terms, 'chip', scatter_dimension=0, tiled=True)]
    all_gather x1 -> x0, blocking collectives: 20.8 us -> none  [local(): lax.all_gather(tokens, 'chip', axis=0, tiled=True)]
    all_to_all x1 -> x0, waiting for transfers between devices: 12.1 us -> none  [local(): lax.all_to_all(result.reshape(received.shape), ('node', 'chip'), split_ax...]
    convert_element_type x2, other arithmetic: 1.69 us -> 8.81 us  [the longest x1 8.8 us: local(): terms = terms.astype(jnp.bfloat16).reshape(experts, tok_rows, model_width)]
    broadcast_in_dim x0 -> x3, local copies, waits for them, and re-layouts: none -> 5.58 us  [local(): terms = terms + jnp.where(own_node[:, None, None], partial_terms[None], 0.0)]
    all_to_all x1 -> x0, starting transfers between devices: 4.22 us -> none  [local(): lax.all_to_all(result.reshape(received.shape), ('node', 'chip'), split_ax...]
  transfers between devices with their start and end apart: 2 -> 0, of which waited for: 2 -> 0; matrix products, arithmetic and copies ran while one was open for 8% -> 0% of each run, Pallas kernels for 0% -> 0%
where the time goes in v1:
time: 110 us
  Pallas kernels  57.1 us (52%)
  matrix products  26.4 us (24%)
  local copies, waits for them, and re-layouts  13.4 us (12%)
  other arithmetic  12.1 us (11%)
    pallas_call x1, Pallas kernels, scatter_sums(): pl.pallas_call(lambda *refs: scatter_kernel(nodes, *refs), out_shape=jax....  31.9 us
    pallas_call x1, Pallas kernels, gather_tokens(): pl.pallas_call(lambda *refs: gather_kernel(nodes, *refs), out_shape=jax.S...  25.2 us
    dot_general x1, matrix products, local(): lax.dot_general(place, result, (((0,), (0,)), ((), ())), preferred_elemen...  9.1 us
    convert_element_type x1, other arithmetic, local(): terms = terms.astype(jnp.bfloat16).reshape(experts, tok_rows, model_width)  8.8 us
    dot_general x2, matrix products, swiglu_hidden(): jnp.dot(token_rows, gate_matrix, preferred_element_type=jnp.float32)  5.84 us
    broadcast_in_dim x3, local copies, waits for them, and re-layouts, local(): terms = terms + jnp.where(own_node[:, None, None], partial_terms[None], 0.0)  5.58 us
    unnamed x23, local copies, waits for them, and re-layouts  5.14 us
    dot_general x1, matrix products, local(): jnp.dot(shared_hidden, shared_down, preferred_element_type=jnp.float32)  4.22 us

profile of v1, /device:TPU:9, one launch (start us, length us, event | category | flops | bytes accessed | tf_op | source)
XLA Modules:
  0.0 109.9 jit_solution(2129708733160855458)
XLA Ops:
  0.7 0.9 copy.20
  1.6 0.8 copy.21
  2.3 0.1 select_reduce_fusion.1
  2.5 1.6 %pad_maximum_fusion.refs_0_ = bf16[16,3712]{1,0:T(8,128)(2,1)} fusion(bf16[16,128]{1,0:T(8,128)(2,1)S(1)} %fusion.41, bf16[16,3584]{1,0:T(8,128)(2,1)} %param.14), kind=kLoop, calls=%fused_computation.36 | loop fusion | flops 237568 | bytes 237568 | tf_op jit(solution)/shard_map/concatenate | solution.py:328
  4.1 25.2 %gather_tokens.1 = bf16[32,16,3712]{2,1,0:T(8,128)(2,1)} custom-call(bf16[16,3712]{1,0:T(8,128)(2,1)} %pad_maximum_fusion.refs_0_), custom_call_target="tpu_custom_call" | custom-call | tf_op jit(solution)/shard_map/gather_tokens/pallas_call | solution.py:179
  29.3 1.0 select_reduce_fusion
  30.4 0.2 reduce_window_sum.11
  30.8 3.3 %convolution_convert_fusion = bf16[256,3584]{1,0:T(8,128)(2,1)S(1)} fusion(s32[512]{0:T(512)S(1)} %broadcast_select_fusion, bf16[512,3712]{1,0:T(8,128)(2,1)} %bitcast.35), kind=kOutput, calls=%fused_computation.10 | convolution fusion | flops 940572672 | bytes 5507072 | tf_op jit(solution)/shard_map/dot_general | solution.py:345
  34.1 5.4 %fusion.5 = f32[256,1024]{1,0:T(8,128)S(1)} fusion(bf16[256,3584]{1,0:T(8,128)(2,1)S(1)} %convolution_convert_fusion, bf16[1,3584,1024]{2,1,0:T(8,128)(2,1)} %param.17), kind=kOutput, calls=%fused_computation.5 | convolution fusion | flops 1879048192 | bytes 10223616 | tf_op jit(solution)/shard_map/dot_general | solution.py:16
  39.6 2.2 %fusion.15 = bf16[256,1024]{1,0:T(8,128)(2,1)S(1)} fusion(bf16[256,3584]{1,0:T(8,128)(2,1)S(1)} %convolution_convert_fusion, bf16[1,3584,1024]{2,1,0:T(8,128)(2,1)S(1)} %bitcast.39, f32[256,1024]{1,0:T(8,128)S(1)} %fusion.5), kind=kOutput, calls=%fused_computation.12 | convolution fusion | flops 1880621056 | bytes 10747904 | tf_op jit(solution)/shard_map/dot_general | solution.py:17
  41.8 9.1 %convolution_multiply_fusion = f32[512,3584]{1,0:T(8,128)} fusion(f32[512]{0:T(512)S(1)} %select_reduce_fusion, bf16[256,1024]{1,0:T(8,128)(2,1)S(1)} %fusion.15, bf16[1,1024,3584]{2,1,0:T(8,128)(2,1)} %param.19, s32[512]{0:T(512)S(1)} %broadcast_select_fusion), kind=kOutput, calls=%fused_computation.8 | convolution fusion | flops 2821455872 | bytes 15208448 | tf_op jit(solution)/shard_map/dot_general | solution.py:349
  50.9 2.4 %slice.9 = bf16[512,3584]{1,0:T(8,128)(2,1)S(1)} slice(bf16[512,3712]{1,0:T(8,128)(2,1)} %bitcast.36), slice={[0:512], [0:3584]} | slice | bytes 7340032 | tf_op jit(solution)/shard_map/slice | solution.py:335
  53.3 1.9 %copy-done.1 = bf16[512,3584]{1,0:T(8,128)(2,1)} copy-done((bf16[512,3584]{1,0:T(8,128)(2,1)}, bf16[512,3584]{1,0:T(8,128)(2,1)S(1)}, u32[]{:S(2)}) %copy-start.1) | copy-done | bytes 3670040
  55.2 0.4 fusion.27
  55.6 4.2 %fusion.24 = f32[128,3584]{1,0:T(8,128)} fusion(bf16[256,3584]{1,0:T(8,128)(2,1)S(1)} %copy-done, bf16[3584,256]{1,0:T(8,128)(2,1)} %param.21, bf16[512,3584]{1,0:T(8,128)(2,1)} %copy-done.1, s32[]{:T(128)S(6)} %select_n.34, f32[128,256]{1,0:T(8,128)S(1)} %fusion.27), kind=kOutput, calls=%fused_computation.22 | convolution fusion | flops 469958656 | bytes 6553604 | tf_op jit(solution)/shard_map/dot_general | solution.py:354
  59.8 5.4 %broadcast_in_dim.89 = f32[4,128,3584]{2,1,0:T(8,128)} broadcast(f32[128,3584]{1,0:T(8,128)} %fusion.24), dimensions={1,2} | broadcast | bytes 9175040 | tf_op jit(solution)/shard_map/jit(_where)/broadcast_in_dim | solution.py:358
  65.4 8.8 %add_convert_fusion.refs_0_ = bf16[32,16,3584]{2,1,0:T(8,128)(2,1)} fusion(f32[32,16,3584]{2,1,0:T(8,128)} %bitcast.37, f32[32,16,3584]{2,1,0:T(8,128)} %bitcast.33, pred[32]{0:T(512)(128)(4,1)S(1)} %broadcast_in_dim.87), kind=kLoop, calls=%fused_computation.7 | loop fusion | flops 5505024 | bytes 18350112 | tf_op jit(solution)/shard_map/convert_element_type | solution.py:359
  74.2 31.9 %scatter_sums.1 = bf16[16,3584]{1,0:T(8,128)(2,1)} custom-call(bf16[32,16,3584]{2,1,0:T(8,128)(2,1)} %add_convert_fusion.refs_0_), custom_call_target="tpu_custom_call" | custom-call | tf_op jit(solution)/shard_map/scatter_sums/pallas_call | solution.py:275
  106.3 0.1 reshape.91
  106.4 0.1 fusion.51
  106.6 0.3 fusion.20
  106.9 0.2 fusion.50
  107.1 1.3 %convolution_convert_fusion.1 = bf16[4,64,512]{2,1,0:T(8,128)(2,1)} fusion(bf16[4,128,512]{2,1,0:T(8,128)(2,1)S(1)} %copy-done.3, f32[4,64]{1,0:T(4,128)S(1)} %fusion.50, f32[4,64,128]{2,1,0:T(8,128)S(1)} %fusion.20, pred[4,128]{1,0:T(4,128)(4,1)S(1)} %iota_compare_fusion.5), kind=kOutput, calls=%fused_computation.13 | convolution fusion | flops 33816960 | bytes 919040 | tf_op jit(solution)/shard_map/shp,spl->shl/dot_general | solution.py:39
  108.3 1.6 %copy.23 = bf16[16,3584]{1,0:T(8,128)(2,1)} copy(bf16[16,3584]{1,0:T(8,128)(2,1)} %scatter_sums.1) | data formatting | bytes 229376
  (33 shorter events, 0.6 us)
Async XLA Ops:
  0.6 55.0 %copy-start = (bf16[256,3584]{1,0:T(8,128)(2,1)S(1)}, bf16[256,3584]{1,0:T(8,128)(2,1)}, u32[]{:S(2)}) copy-start(bf16[256,3584]{1,0:T(8,128)(2,1)} %param.22) | copy-start | bytes 5505028
  30.7 8.8 %slice-start = ((s8[7340032]{0:T(1024)(128)(4,1)}), s8[4194304]{0:T(1024)(128)(4,1)S(1)}, s32[]{:S(2)}) async-start(s8[7340032]{0:T(1024)(128)(4,1)} %bitcast.38), calls=%async_computation | async-start | bytes 8388608
  34.1 5.5 %slice-start.1 = ((s8[7340032]{0:T(1024)(128)(4,1)}), s8[3145728]{0:T(1024)(128)(4,1)S(1)}, s32[]{:S(2)}) async-start(s8[7340032]{0:T(1024)(128)(4,1)} %bitcast.38), calls=%async_computation.1 | async-start | bytes 6291456
  50.9 4.3 %copy-start.2 = (bf16[3584,256]{1,0:T(8,128)(2,1)S(1)}, bf16[3584,256]{1,0:T(8,128)(2,1)}, u32[]{:S(2)}) copy-start(bf16[3584,256]{1,0:T(8,128)(2,1)} %param.20) | copy-start | bytes 5505028
  53.3 1.9 %copy-start.1 = (bf16[512,3584]{1,0:T(8,128)(2,1)}, bf16[512,3584]{1,0:T(8,128)(2,1)S(1)}, u32[]{:S(2)}) copy-start(bf16[512,3584]{1,0:T(8,128)(2,1)S(1)} %slice.9) | copy-start | bytes 11010052
  74.2 32.0 %copy-start.7 = (s32[4]{0:T(128)S(1)}, s32[4]{0:T(128)}, u32[]{:S(2)}) copy-start(s32[4]{0:T(128)} %param.27) | copy-start | bytes 52
  74.2 32.1 %copy-start.6 = (bf16[4,4096]{1,0:T(4,128)(2,1)S(1)}, bf16[4,4096]{1,0:T(4,128)(2,1)}, u32[]{:S(2)}) copy-start(bf16[4,4096]{1,0:T(4,128)(2,1)} %param.24) | copy-start | bytes 98308
  74.2 32.2 %copy-start.5 = (bf16[4,64,128]{2,1,0:T(8,128)(2,1)S(1)}, bf16[4,64,128]{2,1,0:T(8,128)(2,1)}, u32[]{:S(2)}) copy-start(bf16[4,64,128]{2,1,0:T(8,128)(2,1)} %param.26) | copy-start | bytes 196612
  74.2 32.3 %copy-start.3 = (bf16[4,128,512]{2,1,0:T(8,128)(2,1)S(1)}, bf16[4,128,512]{2,1,0:T(8,128)(2,1)}, u32[]{:S(2)}) copy-start(bf16[4,128,512]{2,1,0:T(8,128)(2,1)} %param.25) | copy-start | bytes 1572868
  74.2 32.3 %copy-start.4 = (bf16[4,64,512]{2,1,0:T(8,128)(2,1)S(1)}, bf16[4,64,512]{2,1,0:T(8,128)(2,1)}, u32[]{:S(2)}) copy-start(bf16[4,64,512]{2,1,0:T(8,128)(2,1)} %param.23) | copy-start | bytes 786436

commit v2 on v1

--- a/solution.py
+++ b/solution.py
@@ -289,6 +289,150 @@
         compiler_params=pltpu.CompilerParams(collective_id=1, has_side_effects=True),
         name="scatter_sums",
     )(terms)
+
+
+def expert_kernel(nodes, slots, rows_ref, gate_ref, up_ref, down_ref, sgate_ref, sup_ref, sdown_ref,
+                  out_ref, rows, gate, up, down, sgate, sup, sdown, out, weight, place_t, place,
+                  picked, hidden, rows_sem, gate_sem, up_sem, down_sem, s_sem, sdown_sem, out_sem):
+    total = rows.shape[0]
+    width = down.shape[1]
+    tile_d, tile_f = 512, 256
+    steps_d, steps_f = width // tile_d, gate.shape[1] // tile_f
+    experts = nodes * 8
+    count = total // experts
+    node = lax.axis_index("node")
+    me = node * 8 + lax.axis_index("chip")
+    group = pl.ds(pl.multiple_of(node * 8 * count, 8 * count), 8 * count)
+    tail = pl.ds(width, rows.shape[1] - width)
+    f32, bf16 = jnp.float32, jnp.bfloat16
+
+    def cols(j, tile):
+        return pl.ds(pl.multiple_of(j * tile, tile), tile)
+
+    def part(src, dst, at, sem):
+        return pltpu.make_async_copy(src.at[:, at], dst.at[:, at], sem)
+
+    def rows_part(j):
+        return part(rows_ref, rows, cols(j, tile_d), rows_sem.at[j])
+
+    def gate_part(j):
+        return part(gate_ref, gate, cols(j, tile_f), gate_sem.at[j])
+
+    def up_part(j):
+        return part(up_ref, up, cols(j, tile_f), up_sem.at[j])
+
+    def down_part(j):
+        return part(down_ref, down, cols(j, tile_d), down_sem.at[j])
+
+    def sdown_part(j):
+        return part(sdown_ref, sdown, cols(j, tile_d), sdown_sem.at[j])
+
+    def out_part(j):
+        return part(out, out_ref, cols(j, tile_d), out_sem.at[j])
+
+    tail_copy = part(rows_ref, rows, tail, rows_sem.at[steps_d])
+    sgate_copy = pltpu.make_async_copy(sgate_ref, sgate, s_sem.at[0])
+    sup_copy = pltpu.make_async_copy(sup_ref, sup, s_sem.at[1])
+    tail_copy.start()
+    for j in range(steps_d):
+        rows_part(j).start()
+    for j in range(steps_f):
+        gate_part(j).start()
+        up_part(j).start()
+    sgate_copy.start()
+    sup_copy.start()
+    for j in range(steps_d):
+        down_part(j).start()
+        sdown_part(j).start()
+
+    def dot(first, second):
+        return jnp.dot(first, second, preferred_element_type=f32)
+
+    tail_copy.wait()
+    side = rows[:, tail]
+    lane = lax.broadcasted_iota(jnp.int32, (side.shape[1], LANES), 0)
+    mine = (lane == me) | (lane == experts + me)
+    weight[...] = dot(side, mine.astype(f32).astype(bf16))
+    chosen = weight[...] > 0
+    token = lax.broadcasted_iota(jnp.int32, (total, total), 0)
+    other = lax.broadcasted_iota(jnp.int32, (total, total), 1)
+    ahead = (token // count == other // count) & (other <= token)
+    rank = dot(ahead.astype(f32).astype(bf16), chosen.astype(f32).astype(bf16))
+    block = lax.broadcasted_iota(jnp.int32, (total, LANES), 0) // count
+    slot = jnp.where(chosen, rank.astype(jnp.int32) - 1 + block * slots, -1)
+    for k in range(experts * slots // LANES):
+        spot = lax.broadcasted_iota(jnp.int32, (total, LANES), 1) + k * LANES
+        hit = (slot == spot).astype(f32)
+        place_t[:, k * LANES:(k + 1) * LANES] = hit.astype(bf16)
+        place[k * LANES:(k + 1) * LANES, :] = hit.T.astype(bf16)
+
+    @pl.loop(0, steps_d)
+    def _(j):
+        rows_part(j).wait()
+        at = cols(j, tile_d)
+        picked[:, at] = dot(place[...], rows[:, at]).astype(bf16)
+
+    def glu(gate_sum, up_sum):
+        return (jax.nn.silu(gate_sum) * up_sum).astype(bf16)
+
+    @pl.loop(0, steps_f)
+    def _(j):
+        at = cols(j, tile_f)
+        gate_part(j).wait()
+        gate_sum = dot(picked[...], gate[:, at])
+        up_part(j).wait()
+        hidden[:, at] = glu(gate_sum, dot(picked[...], up[:, at]))
+
+    sgate_copy.wait()
+    sup_copy.wait()
+    near = rows[group, 0:width]
+    shared = glu(dot(near, sgate[...]), dot(near, sup[...]))
+
+    @pl.loop(0, steps_d)
+    def _(j):
+        at = cols(j, tile_d)
+        down_part(j).wait()
+        result = dot(hidden[...], down[:, at]).astype(bf16)
+        sdown_part(j).wait()
+        partial = dot(shared, sdown[:, at])
+        for r in range(nodes):
+            span = slice(r * 8 * count, (r + 1) * 8 * count)
+            terms = dot(place_t[span, :], result) * weight[span, 0:1]
+            terms = terms + jnp.where(node == r, partial, 0.0)
+            out[span, at] = terms.astype(bf16)
+        out_part(j).start()
+
+    for j in range(steps_d):
+        out_part(j).wait()
+
+
+def run_experts(rows, gate, up, down, sgate, sup, sdown, nodes, slots):
+    total = rows.shape[0]
+    width = down.shape[1]
+    count = nodes * 8 * slots
+    steps_d, steps_f = width // 512, gate.shape[1] // 256
+    dma = pltpu.SemaphoreType.DMA
+    bf16 = jnp.bfloat16
+    hold = lambda a: pltpu.VMEM(a.shape, a.dtype)
+    operands = (rows, gate, up, down, sgate, sup, sdown)
+    return pl.pallas_call(
+        lambda *refs: expert_kernel(nodes, slots, *refs),
+        out_shape=jax.ShapeDtypeStruct((total, width), bf16),
+        in_specs=[pl.BlockSpec(memory_space=pl.ANY)] * len(operands),
+        out_specs=pl.BlockSpec(memory_space=pl.ANY),
+        scratch_shapes=[hold(a) for a in operands] + [
+            pltpu.VMEM((total, width), bf16),
+            pltpu.VMEM((total, LANES), jnp.float32),
+            pltpu.VMEM((total, count), bf16),
+            pltpu.VMEM((count, total), bf16),
+            pltpu.VMEM((count, width), bf16),
+            pltpu.VMEM((count, gate.shape[1]), bf16),
+            dma((steps_d + 1,)), dma((steps_f,)), dma((steps_f,)), dma((steps_d,)),
+            dma((2,)), dma((steps_d,)), dma((steps_d,)),
+        ],
+        compiler_params=pltpu.CompilerParams(vmem_limit_bytes=60 * 2**20),
+        name="run_experts",
+    )(*operands)
 
 
 def local(
@@ -331,6 +475,13 @@
     else:
         gathered = lax.all_gather(rows, ("node", "chip"), axis=0)
     total = experts * tok_rows
+    if trees:
+        terms = run_experts(
+            gathered.reshape(total, -1), expert_gate[0], expert_up[0], expert_down[0],
+            shared_gate, shared_up, shared_down, node_count, slots,
+        )
+        moe_out = scatter_sums(terms.reshape(experts, tok_rows, model_width), node_count)
+        return moe_out, attend(query_latent, query_rope, cache_latent, cache_rope, cache_len)
     flat = gathered.reshape(total, -1)
     every = flat[:, :model_width]
     tail = flat[:, model_width:].astype(jnp.float32)
@@ -352,17 +503,13 @@
     group = lax.dynamic_slice_in_dim(every, node * chip_count * tok_rows, chip_count * tok_rows, 0)
     shared_hidden = swiglu_hidden(group, shared_gate, shared_up)
     partial_terms = jnp.dot(shared_hidden, shared_down, preferred_element_type=jnp.float32)
-    in_group = (names // chip_count == node).astype(jnp.float32)
     terms = (spread * scale[:, None]).reshape(node_count, -1, model_width)
     own_node = jnp.arange(node_count) == node
     terms = terms + jnp.where(own_node[:, None, None], partial_terms[None], 0.0)
     terms = terms.astype(jnp.bfloat16).reshape(experts, tok_rows, model_width)
-    if trees:
-        moe_out = scatter_sums(terms, node_count)
-    else:
-        moe_out = lax.psum_scatter(
-            terms.reshape(total, model_width), ("node", "chip"), scatter_dimension=0, tiled=True
-        )
+    moe_out = lax.psum_scatter(
+        terms.reshape(total, model_width), ("node", "chip"), scatter_dimension=0, tiled=True
+    )
     attn_out = attend(query_latent, query_rope, cache_latent, cache_rope, cache_len)
     return (moe_out, attn_out)
 

time: 110 us -> 89.7 us (0.82)
  matrix products: 26.4 us -> 1.73 us
  Pallas kernels: 57.1 us -> 81.7 us
  local copies, waits for them, and re-layouts: 13.4 us -> 3.28 us
  other arithmetic: 12.1 us -> 2.02 us
    dot_general x6 -> x0, matrix products: 24.7 us -> none  [the longest x1 9.1 us: local(): lax.dot_general(place, result, (((0,), (0,)), ((), ())), preferred_elemen...]
    pallas_call x0 -> x1, Pallas kernels: none -> 24.6 us  [run_experts(): pl.pallas_call(lambda *refs: expert_kernel(nodes, slots, *refs), out_shap...]
    convert_element_type x2 -> x0, other arithmetic: 8.81 us -> none  [the longest x1 8.8 us: local(): terms = terms.astype(jnp.bfloat16).reshape(experts, tok_rows, model_width)]
    broadcast_in_dim x3 -> x0, local copies, waits for them, and re-layouts: 5.58 us -> none  [local(): terms = terms + jnp.where(own_node[:, None, None], partial_terms[None], 0.0)]
    slice x1 -> x0, local copies, waits for them, and re-layouts: 2.41 us -> none  [local(): every = flat[:, :model_width]]
    unnamed x23 -> x13, local copies, waits for them, and re-layouts: 5.14 us -> 3.16 us
where the time goes in v2:
time: 89.7 us; the launch traced here: 89.4 us
  Pallas kernels  81.7 us (91%)
  local copies, waits for them, and re-layouts  3.28 us (4%)
  other arithmetic  2.02 us (2%)
  matrix products  1.73 us (2%)
    pallas_call x1, Pallas kernels, scatter_sums(): pl.pallas_call(lambda *refs: scatter_kernel(nodes, *refs), out_shape=jax....  31.9 us
    pallas_call x1, Pallas kernels, gather_tokens(): pl.pallas_call(lambda *refs: gather_kernel(nodes, *refs), out_shape=jax.S...  25.2 us
    pallas_call x1, Pallas kernels, run_experts(): pl.pallas_call(lambda *refs: expert_kernel(nodes, slots, *refs), out_shap...  24.6 us
    unnamed x13, local copies, waits for them, and re-layouts  3.16 us

profile of v2, /device:TPU:9, one launch (start us, length us, event | category | flops | bytes accessed | tf_op | source)
XLA Modules:
  0.0 89.4 jit_solution(14141350546300875080)
XLA Ops:
  0.6 0.0 copy-start
  0.6 0.8 copy.19
  1.5 0.8 copy.18
  2.2 0.1 select_reduce_fusion
  2.3 0.1 fusion.10
  2.4 1.6 %pad_maximum_fusion.refs_0_ = bf16[16,3712]{1,0:T(8,128)(2,1)} fusion(bf16[16,128]{1,0:T(8,128)(2,1)S(1)} %fusion.10, bf16[16,3584]{1,0:T(8,128)(2,1)} %param.14), kind=kLoop, calls=%fused_computation.9 | loop fusion | flops 237568 | bytes 237568 | tf_op jit(solution)/shard_map/concatenate | solution.py:472
  4.0 25.2 %gather_tokens.1 = bf16[32,16,3712]{2,1,0:T(8,128)(2,1)} custom-call(bf16[16,3712]{1,0:T(8,128)(2,1)} %pad_maximum_fusion.refs_0_), custom_call_target="tpu_custom_call" | custom-call | tf_op jit(solution)/shard_map/gather_tokens/pallas_call | solution.py:179
  29.2 24.6 %run_experts.1 = bf16[512,3584]{1,0:T(8,128)(2,1)} custom-call(bf16[512,3712]{1,0:T(8,128)(2,1)} %bitcast.12, bf16[3584,1024]{1,0:T(8,128)(2,1)} %bitcast.14, bf16[3584,1024]{1,0:T(8,128)(2,1)} %bitcast.15, bf16[1024,3584]{1,0:T(8,128)(2,1)} %bitcast.16, bf16[3584,256]{1,0:T(8,128)(2,1)} %refs_4_.1, bf16[3584,256]{1,0:T(8,128)(2,1)} %refs_5_.1, ...), custom_call_target="tpu_custom_call" | custom-call | tf_op jit(solution)/shard_map/run_experts/pallas_call | solution.py:418
  53.8 0.0 copy-start.3
  53.8 0.0 copy-start.2
  53.8 0.0 copy-start.4
  53.8 0.0 copy-start.1
  53.8 31.9 %scatter_sums.1 = bf16[16,3584]{1,0:T(8,128)(2,1)} custom-call(bf16[32,16,3584]{2,1,0:T(8,128)(2,1)} %bitcast.13), custom_call_target="tpu_custom_call" | custom-call | tf_op jit(solution)/shard_map/scatter_sums/pallas_call | solution.py:275
  85.7 0.0 copy-done.3
  85.7 0.1 reshape.40
  85.8 0.0 copy-done.2
  85.9 0.1 fusion.14
  86.0 0.0 copy-done.4
  86.0 0.1 iota_compare_fusion.2
  86.1 0.0 copy-done
  86.1 0.3 fusion.3
  86.4 0.2 fusion.13
  86.6 1.3 %convolution_convert_fusion = bf16[4,64,512]{2,1,0:T(8,128)(2,1)} fusion(bf16[4,128,512]{2,1,0:T(8,128)(2,1)S(1)} %copy-done, f32[4,64]{1,0:T(4,128)S(1)} %fusion.13, f32[4,64,128]{2,1,0:T(8,128)S(1)} %fusion.3, pred[4,128]{1,0:T(4,128)(4,1)S(1)} %iota_compare_fusion.2), kind=kOutput, calls=%fused_computation.1 | convolution fusion | flops 33816960 | bytes 919040 | tf_op jit(solution)/shard_map/shp,spl->shl/dot_general | solution.py:39
  87.9 1.6 %copy.21 = bf16[16,3584]{1,0:T(8,128)(2,1)} copy(bf16[16,3584]{1,0:T(8,128)(2,1)} %scatter_sums.1) | data formatting | bytes 229376
  (2 shorter events, 0.0 us)
Async XLA Ops:
  0.6 85.4 %copy-start = (bf16[4,128,512]{2,1,0:T(8,128)(2,1)S(1)}, bf16[4,128,512]{2,1,0:T(8,128)(2,1)}, u32[]{:S(2)}) copy-start(bf16[4,128,512]{2,1,0:T(8,128)(2,1)} %param.25) | copy-start | bytes 1572868
  53.8 31.9 %copy-start.3 = (bf16[4,4096]{1,0:T(4,128)(2,1)S(1)}, bf16[4,4096]{1,0:T(4,128)(2,1)}, u32[]{:S(2)}) copy-start(bf16[4,4096]{1,0:T(4,128)(2,1)} %param.24) | copy-start | bytes 98308
  53.8 32.0 %copy-start.2 = (bf16[4,64,128]{2,1,0:T(8,128)(2,1)S(1)}, bf16[4,64,128]{2,1,0:T(8,128)(2,1)}, u32[]{:S(2)}) copy-start(bf16[4,64,128]{2,1,0:T(8,128)(2,1)} %param.26) | copy-start | bytes 196612
  53.8 32.2 %copy-start.4 = (s32[4]{0:T(128)S(1)}, s32[4]{0:T(128)}, u32[]{:S(2)}) copy-start(s32[4]{0:T(128)} %param.27) | copy-start | bytes 52
  53.8 32.3 %copy-start.1 = (bf16[4,64,512]{2,1,0:T(8,128)(2,1)S(1)}, bf16[4,64,512]{2,1,0:T(8,128)(2,1)}, u32[]{:S(2)}) copy-start(bf16[4,64,512]{2,1,0:T(8,128)(2,1)} %param.23) | copy-start | bytes 786436
